TPU v7x, 32 devices: a 4x4x1 block of a 4x4x8 slice. The times are simulated.
32 devices in a mesh: dp: 1 (over z), tp: 4 (over y), sq: 8 (over x, core).
Axes of the slice: x: 4, y: 4, z: 1, core: 2. Of those that a mesh axis runs over, the one named last changes fastest.
The devices are a block of a 4x4x8 slice.
Arguments:
- hidden: bfloat16 [256, 2048], P('dp')
- cache_lens: int32 [256], P('dp')
- k_cache: bfloat16 [256, 2048, 128], P('dp', 'sq')
- v_cache: bfloat16 [256, 2048, 128], P('dp', 'sq')
- ln_gain: float32 [2048], replicated
- ln_bias: float32 [2048], replicated
- w_query: bfloat16 [2048, 2048], P(None, 'tp')
- b_query: float32 [2048], P('tp')
- w_kv: bfloat16 [2048, 256], replicated
- b_kv: float32 [256], replicated
- w_out: bfloat16 [2048, 2048], P('tp')
- b_out: float32 [2048], replicated
Outputs:
- output 1: bfloat16 [256, 2048], P('dp')
- output 2: bfloat16 [256, 2048, 128], P('dp', 'sq')
- output 3: bfloat16 [256, 2048, 128], P('dp', 'sq')
All inputs are finite; a program needn't handle non-finite values.
Results may differ from a plain program's by a relative error of at most 0.0034095.
Values sent between devices are 32-bit elements.
A program may use at most 768 MiB of HBM per device.

v0:
```python
import jax
import jax.numpy as jnp
from jax import lax
from jax.sharding import PartitionSpec as P


def layer_norm(x_rows, ln_gain, ln_bias):
    x_wide = x_rows.astype(jnp.float32)
    mean_val = jnp.mean(x_wide, axis=-1, keepdims=True)
    centered = x_wide - mean_val
    variance = jnp.mean(centered * centered, axis=-1, keepdims=True)
    normed = centered * lax.rsqrt(variance + 1e-5)
    return (normed * ln_gain + ln_bias).astype(jnp.bfloat16)


def solution(mesh):
    def local_step(hidden, cache_lens, k_cache, v_cache, ln_gain, ln_bias, w_query, b_query, w_kv, b_kv, w_out, b_out):
        batch, pos_local, head_dim = k_cache.shape
        heads_local = w_query.shape[1] // head_dim
        normed = layer_norm(hidden, ln_gain, ln_bias)
        query = (jnp.dot(normed, w_query, preferred_element_type=jnp.float32) + b_query).astype(jnp.bfloat16)
        query = query.reshape(batch, heads_local, head_dim)
        key_val = (jnp.dot(normed, w_kv, preferred_element_type=jnp.float32) + b_kv).astype(jnp.bfloat16)
        first_pos = lax.axis_index("sq") * pos_local
        positions = first_pos + lax.broadcasted_iota(jnp.int32, (1, pos_local), 1)
        at_slot = (positions == cache_lens[:, None])[:, :, None]
        key_new = jnp.where(at_slot, key_val[:, None, :head_dim], k_cache)
        val_new = jnp.where(at_slot, key_val[:, None, head_dim:], v_cache)
        scores = jnp.einsum("bnd,btd->bnt", query, key_new, preferred_element_type=jnp.float32) * (head_dim ** -0.5)
        valid = (positions <= cache_lens[:, None])[:, None, :]
        scores = jnp.where(valid, scores, -1e30)
        local_max = jnp.max(scores, axis=-1, keepdims=True)
        global_max = lax.pmax(local_max, "sq")
        weights = jnp.where(valid, jnp.exp(scores - global_max), 0.0)
        denominator = lax.psum(jnp.sum(weights, axis=-1, keepdims=True), "sq")
        numerator = lax.psum(jnp.einsum("bnt,btd->bnd", weights.astype(jnp.bfloat16), val_new, preferred_element_type=jnp.float32), "sq")
        attended = (numerator / denominator).astype(jnp.bfloat16).reshape(batch, heads_local * head_dim)
        part_sum = jnp.dot(attended, w_out, preferred_element_type=jnp.float32)
        projected = lax.psum(part_sum, "tp")
        out_hidden = (hidden.astype(jnp.float32) + projected + b_out).astype(jnp.bfloat16)
        return out_hidden, key_new, val_new

    cache_spec = P("dp", "sq", None)
    row_spec = P("dp", None)
    in_specs = (row_spec, P("dp"), cache_spec, cache_spec, P(None), P(None), P(None, "tp"), P("tp"), P(None, None), P(None), P("tp", None), P(None))
    out_specs = (row_spec, cache_spec, cache_spec)
    return jax.shard_map(local_step, mesh=mesh, in_specs=in_specs, out_specs=out_specs, check_vma=False)
```

profile of v0, /device:TPU:97, one launch (start us, length us, event | category | flops | bytes accessed | tf_op | source)
XLA Modules:
  0.0 209.1 jit_solution(13523239375152121679)
XLA Ops:
  7.2 0.0 copy-start
  7.2 0.0 copy-start.1
  7.2 0.0 copy-start.7
  7.2 0.0 copy-start.8
  7.2 0.1 all-reduce.3.cloned.1.call-start
  7.3 0.0 copy-start.6
  7.3 1.6 convert_reduce_fusion
  8.9 1.6 fusion.2
  10.6 0.0 copy-done.1
  10.6 0.0 copy-done.7
  10.6 0.0 copy-start.5
  10.6 0.0 copy-start.9
  10.6 1.4 fusion.10
  12.1 0.1 copy-done.5
  12.2 0.0 copy-done.9
  12.2 1.5 fusion.9
  13.7 1.0 reshape.85
  14.7 0.1 broadcast_compare_fusion.1
  14.9 23.3 %broadcast_select_fusion.1 = (bf16[256,256,128]{2,1,0:T(8,128)(2,1)}, bf16[256,256,128]{2,1,0:T(8,128)(2,1)}) fusion(bf16[256,256,128]{2,1,0:T(8,128)(2,1)} %param.14, pred[256,256]{1,0:T(8,128)(4,1)S(1)} %get-tuple-element.8, bf16[256,128]{1,0:T(8,128)(2,1)S(1)} %get-tuple-element.3, bf16[256,256,128]{2,1,0:T(8,128)(2,1)} %param.15, ...), kind=kLoop, calls=%fused_computation.1 | loop fusion | flops 16777216 | bytes 67305472 | tf_op jit(solution)/shard_map/jit(_where)/select_n | solution.py:27
  38.2 11.0 %fusion.25 = (f32[256,4]{1,0:T(8,128)}, f32[256,4,256]{2,1,0:T(4,128)S(1)}) fusion(bf16[256,4,128]{2,1,0:T(4,128)(2,1)S(1)} %reshape.85, bf16[256,256,128]{2,1,0:T(8,128)(2,1)} %get-tuple-element.5, pred[256,256]{1,0:T(8,128)(4,1)S(1)} %get-tuple-element.7), kind=kOutput, calls=%fused_computation.37 | convolution fusion | flops 67894272 | bytes 18157568 | tf_op jit(solution)/shard_map/bnd,btd->bnt/dot_general | solution.py:29
  49.1 25.7 %pmax.7 = f32[256,4]{1,0:T(8,128)S(1)} all-reduce(f32[256,4]{1,0:T(8,128)} %get-tuple-element.9), channel_id=1, replica_groups=mesh['dp'=1,'tp'=4,'sq'=8] {'sq'}, use_global_device_ids=true, to_apply=%region_3.4 | all-reduce | flops 1024 | bytes 8192 | tf_op jit(solution)/shard_map/pmax | solution.py:33
  74.9 8.9 %fusion.13 = f32[256,4,128]{2,1,0:T(4,128)} fusion(bf16[256,256,128]{2,1,0:T(8,128)(2,1)} %get-tuple-element.6, f32[256,4,256]{2,1,0:T(4,128)S(1)} %get-tuple-element.10, f32[256,4]{1,0:T(8,128)S(1)} %pmax.7, pred[256,256]{1,0:T(8,128)(4,1)S(1)} %get-tuple-element.7), kind=kOutput, calls=%fused_computation.22 | convolution fusion | flops 67895296 | bytes 18419712 | tf_op jit(solution)/shard_map/bnt,btd->bnd/dot_general | solution.py:36
  83.8 0.1 all-reduce.3.cloned.1.call-update
  83.8 0.1 all-reduce.5.cloned.1.call-start
  83.9 0.8 fusion.11
  84.7 25.9 %psum.22 = f32[256,4]{1,0:T(8,128)S(1)} all-reduce(f32[256,4]{1,0:T(8,128)S(1)} %fusion.11), channel_id=1, replica_groups=mesh['dp'=1,'tp'=4,'sq'=8] {'sq'}, use_global_device_ids=true, to_apply=%region_6.7 | all-reduce | flops 1024 | bytes 8192 | tf_op jit(solution)/shard_map/psum | solution.py:35
  110.6 30.7 %all-reduce.3.cloned.1.call-done = f32[256,4,128]{2,1,0:T(4,128)} async-done(((f32[256,4,128]{2,1,0:T(4,128)}), f32[256,4,128]{2,1,0:T(4,128)}) %all-reduce.3.cloned.1.call-update) | async-done | bytes 524304 | tf_op jit(solution)/shard_map/psum | solution.py:36
  141.3 1.4 divide_convert_fusion
  142.7 2.0 fusion.18
  144.7 0.1 all-reduce.5.cloned.1.call-update
  144.7 54.6 %all-reduce.5.cloned.1.call-done = f32[256,2048]{1,0:T(8,128)} async-done(((f32[256,2048]{1,0:T(8,128)}), f32[256,2048]{1,0:T(8,128)}) %all-reduce.5.cloned.1.call-update) | async-done | bytes 2097168 | tf_op jit(solution)/shard_map/psum | solution.py:39
  199.4 2.9 %fusion.7 = bf16[256,2048]{1,0:T(8,128)(2,1)} fusion(f32[256,2048]{1,0:T(8,128)} %all-reduce.5.cloned.1.call-done, bf16[256,2048]{1,0:T(8,128)(2,1)S(1)} %copy-done.2, f32[2048]{0:T(1024)S(1)} %copy-done.3), kind=kLoop, calls=%fused_computation.12 | loop fusion | flops 2097152 | bytes 4202496 | tf_op jit(solution)/shard_map/convert_element_type | solution.py:40
  (13 shorter events, 0.0 us)
Async XLA Ops:
  7.2 135.5 %copy-start = (bf16[512,2048]{1,0:T(8,128)(2,1)S(1)}, bf16[512,2048]{1,0:T(8,128)(2,1)}, u32[]{:S(2)}) copy-start(bf16[512,2048]{1,0:T(8,128)(2,1)} %param.22) | copy-start | bytes 6291460
  7.2 3.4 %copy-start.1 = (bf16[256,2048]{1,0:T(8,128)(2,1)S(1)}, bf16[256,2048]{1,0:T(8,128)(2,1)}, u32[]{:S(2)}) copy-start(bf16[256,2048]{1,0:T(8,128)(2,1)} %param.12) | copy-start | bytes 3145732
  7.2 3.4 %copy-start.7 = (f32[2048]{0:T(1024)S(1)}, f32[2048]{0:T(1024)}, u32[]{:S(2)}) copy-start(f32[2048]{0:T(1024)} %param.17) | copy-start | bytes 24580
  7.2 3.4 %copy-start.8 = (f32[2048]{0:T(1024)S(1)}, f32[2048]{0:T(1024)}, u32[]{:S(2)}) copy-start(f32[2048]{0:T(1024)} %param.16) | copy-start | bytes 24580
  7.2 134.0 %all-reduce.3.cloned.1.call-start = ((), (), s32[]{:S(2)}) async-start(), calls=%async_computation | async-start | bytes 1048576 | tf_op jit(solution)/shard_map/psum | solution.py:36
  7.3 3.3 %copy-start.6 = (bf16[2048,256]{1,0:T(8,128)(2,1)S(1)}, bf16[2048,256]{1,0:T(8,128)(2,1)}, u32[]{:S(2)}) copy-start(bf16[2048,256]{1,0:T(8,128)(2,1)} %param.20) | copy-start | bytes 3145732
  10.6 1.6 copy-start.5
  10.6 1.6 copy-start.9
  12.2 2.5 %copy-start.4 = (s32[256]{0:T(256)S(1)}, s32[256]{0:T(256)}, u32[]{:S(2)}) copy-start(s32[256]{0:T(256)} %param.13) | copy-start | bytes 3076
  83.8 115.5 %all-reduce.5.cloned.1.call-start = ((), (), s32[]{:S(2)}) async-start(), calls=%async_computation.1 | async-start | bytes 4194304 | tf_op jit(solution)/shard_map/psum | solution.py:39
  144.7 54.7 %copy-start.2 = (bf16[256,2048]{1,0:T(8,128)(2,1)S(1)}, bf16[256,2048]{1,0:T(8,128)(2,1)}, u32[]{:S(2)}) copy-start(bf16[256,2048]{1,0:T(8,128)(2,1)} %param.12) | copy-start | bytes 3145732
  144.7 54.7 %copy-start.3 = (f32[2048]{0:T(1024)S(1)}, f32[2048]{0:T(1024)}, u32[]{:S(2)}) copy-start(f32[2048]{0:T(1024)} %param.23) | copy-start | bytes 24580
Sparse Core Ops, SparseCore 0:
  84.0 57.2 all-reduce.2
  144.9 54.4 all-reduce.4
where the time goes:
time: 209 us
  waiting for transfers between devices  85.4 us (41%)
  blocking collectives  51.6 us (25%)
  other arithmetic  31.7 us (15%)
  matrix products  24.8 us (12%)
  between operations  14.3 us (7%)
    psum x1, waiting for transfers between devices, local_step(): projected = lax.psum(part_sum, 'tp')  54.6 us
    psum x1, waiting for transfers between devices, local_step(): lax.psum(jnp.einsum('bnt,btd->bnd', weights.astype(jnp.bfloat16), val_new...  30.7 us
    psum x1, blocking collectives, local_step(): denominator = lax.psum(jnp.sum(weights, axis=-1, keepdims=True), 'sq')  25.9 us
    pmax x1, blocking collectives, local_step(): global_max = lax.pmax(local_max, 'sq')  25.7 us
    select_n x1, other arithmetic, local_step(): key_new = jnp.where(at_slot, key_val[:, None, :head_dim], k_cache)  23.3 us
    dot_general x1, matrix products, local_step(): jnp.einsum('bnd,btd->bnt', query, key_new, preferred_element_type=jnp.flo...  11 us
    dot_general x1, matrix products, local_step(): jnp.einsum('bnt,btd->bnd', weights.astype(jnp.bfloat16), val_new, preferr...  8.91 us
  transfers between devices with their start and end apart: 2, of which 2 were waited for; matrix products, arithmetic and copies ran while one was open for 0% of the time, Pallas kernels for 0%

commit v1 on v0

v1 whole, which is shorter than its diff:
```python
import functools
import jax
import jax.numpy as jnp
from jax import lax
from jax.sharding import PartitionSpec as P
from jax.experimental import pallas as pl
from jax.experimental.pallas import tpu as pltpu

F32 = jnp.float32
BF16 = jnp.bfloat16
MESH = pl.DeviceIdType.MESH
CHUNK = 16
LOW = -1e30


def attend_kernel(lens, hid_h, gain, bias, wq_h, bq, wkv_h, bkv, k_in, v_in,
                  k_out, v_out, num, stat,
                  hid, wq, wkv, h_scr, kv_scr, qd, kbuf, vbuf, wsem, ksem, vsem, kosem, vosem):
    batch, pos, dim = k_in.shape
    heads = wq.shape[1] // dim
    chunks = batch // CHUNK
    first = lax.axis_index("sq") * pos

    wcopies = [pltpu.make_async_copy(src, dst, wsem.at[i])
               for i, (src, dst) in enumerate(((hid_h, hid), (wkv_h, wkv), (wq_h, wq)))]

    def rd(c, src, buf, sem):
        part = pl.ds(c * CHUNK, CHUNK)
        return pltpu.make_async_copy(src.at[part], buf.at[part], sem.at[c])

    def wr(c, buf, dst, sem):
        part = pl.ds(c * CHUNK, CHUNK)
        return pltpu.make_async_copy(buf.at[part], dst.at[part], sem.at[c])

    for copy in wcopies:
        copy.start()
    for c in range(chunks):
        rd(c, k_in, kbuf, ksem).start()
        rd(c, v_in, vbuf, vsem).start()

    wcopies[0].wait()
    rows = 32

    def norm_rows(i, _):
        part = pl.ds(pl.multiple_of(i * rows, rows), rows)
        wide = hid[part, :].astype(F32)
        mean = jnp.mean(wide, axis=-1, keepdims=True)
        cent = wide - mean
        var = jnp.mean(cent * cent, axis=-1, keepdims=True)
        normed = cent * lax.rsqrt(var + 1e-5)
        h_scr[part, :] = (normed * gain[...] + bias[...]).astype(BF16)
        return 0

    lax.fori_loop(0, batch // rows, norm_rows, 0)
    wcopies[1].wait()
    kv = jnp.dot(h_scr[...], wkv[...], preferred_element_type=F32) + bkv[...]
    kv_scr[...] = kv.astype(BF16).astype(F32)
    wcopies[2].wait()
    qd[...] = jnp.zeros_like(qd)
    for h in range(heads):
        cols = slice(h * dim, (h + 1) * dim)
        q = jnp.dot(h_scr[...], wq[:, cols], preferred_element_type=F32) + bq[:, cols]
        q = q.astype(BF16).astype(F32).reshape(batch // 2, 2, dim)
        qd[:, h, 0:dim] = q[:, 0, :]
        qd[:, heads + h, dim:2 * dim] = q[:, 1, :]

    pair_rows = 2 * heads
    row = lax.broadcasted_iota(jnp.int32, (pair_rows, pos), 0)
    at = first + lax.broadcasted_iota(jnp.int32, (pair_rows, pos), 1)
    tile_row = lax.broadcasted_iota(jnp.int32, (16, dim), 0)
    lane = lax.broadcasted_iota(jnp.int32, (pair_rows, dim), 1)
    low_half = lax.broadcasted_iota(jnp.int32, (pair_rows, dim), 0) < heads

    def step(c, _):
        rd(c, k_in, kbuf, ksem).wait()
        rd(c, v_in, vbuf, vsem).wait()
        base = c * CHUNK
        patched = []
        for i in range(CHUNK):
            slot = lens[base + i] - first
            start = pl.multiple_of((jnp.clip(slot, 0, pos - 1) // 16) * 16, 16)
            hit = tile_row + start == slot
            new = kv_scr[pl.ds(base + i, 1), :]
            kt = kbuf[base + i, pl.ds(start, 16), :].astype(F32)
            vt = vbuf[base + i, pl.ds(start, 16), :].astype(F32)
            patched.append((start, jnp.where(hit, new[:, :dim], kt).astype(BF16),
                            jnp.where(hit, new[:, dim:], vt).astype(BF16)))
        for i, (start, kt, vt) in enumerate(patched):
            kbuf[base + i, pl.ds(start, 16), :] = kt
            vbuf[base + i, pl.ds(start, 16), :] = vt
        wr(c, kbuf, k_out, kosem).start()
        wr(c, vbuf, v_out, vosem).start()
        scores = []
        for p in range(CHUNK // 2):
            b = base + 2 * p
            keys = jnp.concatenate([kbuf[b], kbuf[b + 1]], axis=1)
            lhs = qd[c * (CHUNK // 2) + p].astype(BF16)
            s = lax.dot_general(lhs, keys, (((1,), (1,)), ((), ())), preferred_element_type=F32)
            scores.append(s * (dim ** -0.5))
        parts = []
        for p in range(CHUNK // 2):
            b = base + 2 * p
            valid = at <= jnp.where(row < heads, lens[b], lens[b + 1])
            s = jnp.where(valid, scores[p], LOW)
            m = jnp.max(s, axis=-1, keepdims=True)
            w = jnp.where(valid, jnp.exp(s - m), 0.0)
            total = jnp.sum(w, axis=-1, keepdims=True)
            parts.append((m, total, w.astype(BF16)))
        for p in range(CHUNK // 2):
            b = base + 2 * p
            m, total, w = parts[p]
            vals = jnp.concatenate([vbuf[b], vbuf[b + 1]], axis=1)
            o = jnp.dot(w, vals, preferred_element_type=F32)
            out = pl.ds(pl.multiple_of(b * heads, pair_rows), pair_rows)
            num[out, :] = jnp.where(low_half, o[:, :dim], o[:, dim:])
            stat[out, :] = jnp.where(lane == 0, m, total)
        return 0

    lax.fori_loop(0, chunks, step, 0)
    for c in range(chunks):
        wr(c, kbuf, k_out, kosem).wait()
        wr(c, vbuf, v_out, vosem).wait()


def attend(cache_lens, hidden, ln_gain, ln_bias, w_query, b_query, w_kv, b_kv, k_cache, v_cache):
    batch, pos, dim = k_cache.shape
    width = hidden.shape[1]
    heads = w_query.shape[1] // dim
    chunks = batch // CHUNK
    vm = pl.BlockSpec(memory_space=pltpu.VMEM)
    anyw = pl.BlockSpec(memory_space=pl.ANY)
    dma = pltpu.SemaphoreType.DMA
    return pl.pallas_call(
        attend_kernel,
        in_specs=[pl.BlockSpec(memory_space=pltpu.SMEM), anyw, vm, vm, anyw, vm, anyw, vm, anyw, anyw],
        out_specs=[anyw, anyw, vm, vm],
        out_shape=[jax.ShapeDtypeStruct(k_cache.shape, k_cache.dtype),
                   jax.ShapeDtypeStruct(v_cache.shape, v_cache.dtype),
                   jax.ShapeDtypeStruct((batch * heads, dim), F32),
                   jax.ShapeDtypeStruct((batch * heads, dim), F32)],
        scratch_shapes=[
            pltpu.VMEM(hidden.shape, BF16), pltpu.VMEM(w_query.shape, BF16), pltpu.VMEM(w_kv.shape, BF16),
            pltpu.VMEM(hidden.shape, BF16), pltpu.VMEM((batch, 2 * dim), F32),
            pltpu.VMEM((batch // 2, 2 * heads, 2 * dim), F32),
            pltpu.VMEM(k_cache.shape, BF16), pltpu.VMEM(v_cache.shape, BF16),
            dma((3,)), dma((chunks,)), dma((chunks,)), dma((chunks,)), dma((chunks,)),
        ],
        compiler_params=pltpu.CompilerParams(vmem_limit_bytes=54 << 20),
        cost_estimate=pl.CostEstimate(flops=2 * batch * pos * dim * heads * 4, bytes_accessed=4 * k_cache.size * 2, transcendentals=0),
        name="attend",
    )(cache_lens, hidden, ln_gain.reshape(1, -1), ln_bias.reshape(1, -1), w_query, b_query.reshape(1, -1),
      w_kv, b_kv.reshape(1, -1), k_cache, v_cache)


def solution(mesh):
    def local_step(hidden, cache_lens, k_cache, v_cache, ln_gain, ln_bias, w_query, b_query, w_kv, b_kv, w_out, b_out):
        batch, pos, dim = k_cache.shape
        heads = w_query.shape[1] // dim
        key_new, val_new, num, stat = attend(cache_lens, hidden, ln_gain, ln_bias, w_query, b_query, w_kv, b_kv, k_cache, v_cache)
        m, total = stat[:, 0:1], stat[:, 1:2]
        top = lax.pmax(m, "sq")
        f = jnp.exp(m - top)
        den = lax.psum(total * f, "sq")
        numer = lax.psum(num * f, "sq")
        att = (numer / den).astype(BF16).reshape(batch, heads * dim)
        projected = lax.psum(jnp.dot(att, w_out, preferred_element_type=F32), "tp")
        out_hidden = (hidden.astype(F32) + projected + b_out).astype(BF16)
        return out_hidden, key_new, val_new

    cache_spec = P("dp", "sq", None)
    row_spec = P("dp", None)
    in_specs = (row_spec, P("dp"), cache_spec, cache_spec, P(None), P(None), P(None, "tp"), P("tp"), P(None, None), P(None), P("tp", None), P(None))
    return jax.shard_map(local_step, mesh=mesh, in_specs=in_specs, out_specs=(row_spec, cache_spec, cache_spec), check_vma=False)
```

time: 209 us -> 194 us (0.928)
  Pallas kernels: 0 us -> 28 us
  other arithmetic: 31.7 us -> 6.81 us
  matrix products: 24.8 us -> 2.01 us
  waiting for transfers between devices: 85.4 us -> 96.4 us
  blocking collectives: 51.6 us -> 45.7 us
    pallas_call x0 -> x1, Pallas kernels: none -> 28 us  [attend(): pl.pallas_call(attend_kernel, in_specs=[pl.BlockSpec(memory_space=pltpu.S...]
    select_n x1 -> x0, other arithmetic: 23.3 us -> none  [local_step(): key_new = jnp.where(at_slot, key_val[:, None, :head_dim], k_cache)]
    dot_general x5 -> x1, matrix products: 24.8 us -> 2.01 us  [local_step(): projected = lax.psum(jnp.dot(att, w_out, preferred_element_type=F32), 'tp')]
    psum x2, waiting for transfers between devices: 85.3 us -> 96.3 us  [the longest x1 54.6 us: local_step(): projected = lax.psum(jnp.dot(att, w_out, preferred_element_type=F32), 'tp')]
    psum x1, blocking collectives: 25.9 us -> 15.7 us  [local_step(): den = lax.psum(total * f, 'sq')]
    pmax x1, blocking collectives: 25.7 us -> 30 us  [local_step(): top = lax.pmax(m, 'sq')]
    reduce_sum x3 -> x0, other arithmetic: 4.01 us -> none  [the longest x1 1.64 us: layer_norm(): variance = jnp.mean(centered * centered, axis=-1, keepdims=True)]
    mul x0 -> x2, other arithmetic: none -> 2.69 us  [the longest x1 1.7 us: local_step(): den = lax.psum(total * f, 'sq')]
where the time goes in v1:
time: 194 us; the launch traced here: 193 us
  waiting for transfers between devices  96.4 us (50%)
  blocking collectives  45.7 us (24%)
  Pallas kernels  28 us (14%)
  between operations  14.1 us (7%)
  other arithmetic  6.81 us (4%)
  matrix products  2.01 us (1%)
    psum x1, waiting for transfers between devices, local_step(): projected = lax.psum(jnp.dot(att, w_out, preferred_element_type=F32), 'tp')  54.6 us
    psum x1, waiting for transfers between devices, local_step(): numer = lax.psum(num * f, 'sq')  41.6 us
    pmax x1, blocking collectives, local_step(): top = lax.pmax(m, 'sq')  30 us
    pallas_call x1, Pallas kernels, attend(): pl.pallas_call(attend_kernel, in_specs=[pl.BlockSpec(memory_space=pltpu.S...  28 us
    psum x1, blocking collectives, local_step(): den = lax.psum(total * f, 'sq')  15.7 us
  transfers between devices with their start and end apart: 2, of which 2 were waited for; matrix products, arithmetic and copies ran while one was open for 0% of the time, Pallas kernels for 0%

profile of v1, /device:TPU:97, one launch (start us, length us, event | category | flops | bytes accessed | tf_op | source)
XLA Modules:
  0.0 193.3 jit_solution(1634233566367835494)
XLA Ops:
  7.2 0.0 copy-start
  7.2 0.1 all-reduce.3.cloned.1.call-start
  7.3 28.0 %attend.1 = (bf16[256,256,128]{2,1,0:T(8,128)(2,1)}, bf16[256,256,128]{2,1,0:T(8,128)(2,1)}, f32[1024,128]{1,0:T(8,128)}, f32[1024,128]{1,0:T(8,128)}) custom-call(s32[256]{0:T(256)} %lens.1, bf16[256,2048]{1,0:T(8,128)(2,1)} %hid_h.1, f32[1,2048]{1,0:T(1,128)} %bitcast.8, f32[1,2048]{1,0:T(1,128)} %bitcast.9, bf16[2048,512]{1,0:T(8,128)(2,1)} %wq_h.1, ...), custom_call_target="tpu_custom_call" | custom-call | flops 268435456 | bytes 67108864 | tf_op jit(solution)/shard_map/attend/pallas_call | solution.py:133
  35.2 0.0 copy-start.2
  35.2 30.0 %pmax.7 = f32[1024,1]{1,0:T(8,128)S(1)} all-reduce(f32[1024,1]{1,0:T(8,128)} %bitcast.7), channel_id=1, replica_groups=mesh['dp'=1,'tp'=4,'sq'=8] {'sq'}, use_global_device_ids=true, to_apply=%region_0.0 | all-reduce | flops 1024 | bytes 8192 | tf_op jit(solution)/shard_map/pmax | solution.py:161
  65.2 1.7 multiply_reduce_fusion
  66.9 0.0 copy-done.2
  66.9 1.0 broadcast_multiply_fusion
  67.9 0.1 all-reduce.3.cloned.1.call-update
  68.0 0.1 all-reduce.5.cloned.1.call-start
  68.1 15.7 %psum.22 = f32[1024]{0:T(1024)S(1)} all-reduce(f32[1024]{0:T(1024)S(1)} %get-tuple-element.11), channel_id=1, replica_groups=mesh['dp'=1,'tp'=4,'sq'=8] {'sq'}, use_global_device_ids=true, to_apply=%region_2.0 | all-reduce | flops 1024 | bytes 8192 | tf_op jit(solution)/shard_map/psum | solution.py:163
  83.8 41.6 %all-reduce.3.cloned.1.call-done = f32[1024,128]{1,0:T(8,128)} async-done(((f32[1024,128]{1,0:T(8,128)}), f32[1024,128]{1,0:T(8,128)}) %all-reduce.3.cloned.1.call-update) | async-done | bytes 524304 | tf_op jit(solution)/shard_map/psum | solution.py:164
  125.4 1.2 divide_convert_fusion
  126.7 0.2 reshape.26
  126.9 0.0 copy-done
  126.9 2.0 %fusion.1 = f32[256,2048]{1,0:T(8,128)} fusion(bf16[256,512]{1,0:T(8,128)(2,1)S(1)} %reshape.26, bf16[512,2048]{1,0:T(8,128)(2,1)S(1)} %copy-done), kind=kOutput, calls=%fused_computation.6 | convolution fusion | flops 536870912 | bytes 4456448 | tf_op jit(solution)/shard_map/dot_general | solution.py:166
  128.9 0.0 copy-start.1
  128.9 0.0 copy-start.3
  128.9 0.1 all-reduce.5.cloned.1.call-update
  128.9 54.6 %all-reduce.5.cloned.1.call-done = f32[256,2048]{1,0:T(8,128)} async-done(((f32[256,2048]{1,0:T(8,128)}), f32[256,2048]{1,0:T(8,128)}) %all-reduce.5.cloned.1.call-update) | async-done | bytes 2097168 | tf_op jit(solution)/shard_map/psum | solution.py:166
  183.6 0.0 copy-done.1
  183.6 0.0 copy-done.3
  183.6 2.9 %add_convert_fusion = bf16[256,2048]{1,0:T(8,128)(2,1)} fusion(f32[256,2048]{1,0:T(8,128)} %all-reduce.5.cloned.1.call-done, bf16[256,2048]{1,0:T(8,128)(2,1)S(1)} %copy-done.1, f32[2048]{0:T(1024)S(1)} %copy-done.3), kind=kLoop, calls=%fused_computation | loop fusion | flops 2097152 | bytes 4202496 | tf_op jit(solution)/shard_map/convert_element_type | solution.py:167
Async XLA Ops:
  7.2 119.7 %copy-start = (bf16[512,2048]{1,0:T(8,128)(2,1)S(1)}, bf16[512,2048]{1,0:T(8,128)(2,1)}, u32[]{:S(2)}) copy-start(bf16[512,2048]{1,0:T(8,128)(2,1)} %param.22) | copy-start | bytes 6291460
  7.2 118.2 %all-reduce.3.cloned.1.call-start = ((), (), s32[]{:S(2)}) async-start(), calls=%async_computation | async-start | bytes 1048576 | tf_op jit(solution)/shard_map/psum | solution.py:164
  35.2 31.7 %copy-start.2 = (f32[1024,128]{1,0:T(8,128)S(1)}, f32[1024,128]{1,0:T(8,128)}, u32[]{:S(2)}) copy-start(f32[1024,128]{1,0:T(8,128)} %get-tuple-element.7) | copy-start | bytes 1572868
  68.0 115.6 %all-reduce.5.cloned.1.call-start = ((), (), s32[]{:S(2)}) async-start(), calls=%async_computation.1 | async-start | bytes 4194304 | tf_op jit(solution)/shard_map/psum | solution.py:166
  128.9 54.7 %copy-start.1 = (bf16[256,2048]{1,0:T(8,128)(2,1)S(1)}, bf16[256,2048]{1,0:T(8,128)(2,1)}, u32[]{:S(2)}) copy-start(bf16[256,2048]{1,0:T(8,128)(2,1)} %hid_h.1) | copy-start | bytes 3145732
  128.9 54.7 %copy-start.3 = (f32[2048]{0:T(1024)S(1)}, f32[2048]{0:T(1024)}, u32[]{:S(2)}) copy-start(f32[2048]{0:T(1024)} %param.23) | copy-start | bytes 24580
Sparse Core Ops, SparseCore 0:
  68.1 57.2 all-reduce.2
  129.1 54.4 all-reduce.4

commit v2 on v1

v2 whole, which is shorter than its diff:
```python
import functools
import jax
import jax.numpy as jnp
from jax import lax
from jax.sharding import PartitionSpec as P
from jax.experimental import pallas as pl
from jax.experimental.pallas import tpu as pltpu

F32 = jnp.float32
BF16 = jnp.bfloat16
MESH = pl.DeviceIdType.MESH
CHUNK = 16
GROUPS = 4
LOW = -1e30


def attend_kernel(n_sq, lens, hid_h, gain, bias, wq_h, bq, wkv_h, bkv, k_in, v_in,
                  k_out, v_out, msg,
                  hid, wq, wkv, h_scr, kv_scr, qd, stat, k_vm, v_vm, wsem, ksem, vsem, kosem, vosem):
    batch, pos, dim = k_in.shape
    heads = wq.shape[1] // dim
    chunks = batch // CHUNK
    per_group = batch // GROUPS
    own = per_group // n_sq
    rows = own * heads
    first = lax.axis_index("sq") * pos

    wcopies = [pltpu.make_async_copy(src, dst, wsem.at[i])
               for i, (src, dst) in enumerate(((hid_h, hid), (wkv_h, wkv), (wq_h, wq)))]

    def rd(i, src, buf, sem):
        span = pl.ds(i * CHUNK, CHUNK)
        return pltpu.make_async_copy(src.at[span], buf.at[span], sem.at[i])

    def wr(i, buf, dst, sem):
        span = pl.ds(i * CHUNK, CHUNK)
        return pltpu.make_async_copy(buf.at[span], dst.at[span], sem.at[i])

    for copy in wcopies:
        copy.start()
    for i in range(chunks):
        rd(i, k_in, k_vm, ksem).start()
        rd(i, v_in, v_vm, vsem).start()

    wcopies[0].wait()
    nrow = 32

    def norm_rows(i, _):
        span = pl.ds(pl.multiple_of(i * nrow, nrow), nrow)
        wide = hid[span, :].astype(F32)
        mean = jnp.mean(wide, axis=-1, keepdims=True)
        cent = wide - mean
        var = jnp.mean(cent * cent, axis=-1, keepdims=True)
        normed = cent * lax.rsqrt(var + 1e-5)
        h_scr[span, :] = (normed * gain[...] + bias[...]).astype(BF16)
        return 0

    lax.fori_loop(0, batch // nrow, norm_rows, 0)
    wcopies[1].wait()
    kv = jnp.dot(h_scr[...], wkv[...], preferred_element_type=F32) + bkv[...]
    kv_scr[...] = kv.astype(BF16).astype(F32)
    wcopies[2].wait()
    qd[...] = jnp.zeros_like(qd)
    for h in range(heads):
        span = slice(h * dim, (h + 1) * dim)
        q = jnp.dot(h_scr[...], wq[:, span], preferred_element_type=F32) + bq[:, span]
        q = q.astype(BF16).astype(F32).reshape(batch // 2, 2, dim)
        qd[:, h, 0:dim] = q[:, 0, :]
        qd[:, heads + h, dim:2 * dim] = q[:, 1, :]

    pair_rows = 2 * heads
    row = lax.broadcasted_iota(jnp.int32, (pair_rows, pos), 0)
    at = first + lax.broadcasted_iota(jnp.int32, (pair_rows, pos), 1)
    tile_row = lax.broadcasted_iota(jnp.int32, (16, dim), 0)
    lane = lax.broadcasted_iota(jnp.int32, (pair_rows, dim), 1)
    low_half = lax.broadcasted_iota(jnp.int32, (pair_rows, dim), 0) < heads
    pairs = CHUNK // 2
    scale = dim ** -0.5
    per = per_group // CHUNK
    block = dim // rows

    def attend(i, _):
        rd(i, k_in, k_vm, ksem).wait()
        rd(i, v_in, v_vm, vsem).wait()
        base = i * CHUNK
        grp = i // per
        tiles = []
        for j in range(CHUNK):
            slot = lens[base + j] - first
            start = pl.multiple_of((jnp.clip(slot, 0, pos - 1) // 16) * 16, 16)
            hit = tile_row + start == slot
            new = kv_scr[pl.ds(base + j, 1), :]
            kt = k_vm[base + j, pl.ds(start, 16), :].astype(F32)
            vt = v_vm[base + j, pl.ds(start, 16), :].astype(F32)
            tiles.append((start, jnp.where(hit, new[:, :dim], kt).astype(BF16),
                          jnp.where(hit, new[:, dim:], vt).astype(BF16)))
        for j, (start, kt, vt) in enumerate(tiles):
            k_vm[base + j, pl.ds(start, 16), :] = kt
            v_vm[base + j, pl.ds(start, 16), :] = vt
        wr(i, k_vm, k_out, kosem).start()
        wr(i, v_vm, v_out, vosem).start()
        scores = []
        for p in range(pairs):
            b = base + 2 * p
            keys = jnp.concatenate([k_vm[b], k_vm[b + 1]], axis=1)
            q = qd[i * pairs + p].astype(BF16)
            scores.append(lax.dot_general(q, keys, (((1,), (1,)), ((), ())), preferred_element_type=F32) * scale)
        weights = []
        for p in range(pairs):
            b = base + 2 * p
            valid = at <= jnp.where(row < heads, lens[b], lens[b + 1])
            sc = jnp.where(valid, scores[p], LOW)
            m = jnp.max(sc, axis=-1, keepdims=True)
            w = jnp.where(valid, jnp.exp(sc - m), 0.0)
            weights.append((m, jnp.sum(w, axis=-1, keepdims=True), w.astype(BF16)))
        for p in range(pairs):
            b = base + 2 * p
            m, total, w = weights[p]
            vals = jnp.concatenate([v_vm[b], v_vm[b + 1]], axis=1)
            o = jnp.dot(w, vals, preferred_element_type=F32)
            j = lax.rem(b, per_group)
            msg[grp, j // own, pl.ds(pl.multiple_of(lax.rem(j, own) * heads, pair_rows), pair_rows), :] = jnp.where(low_half, o[:, :dim], o[:, dim:])
            stat[pl.ds(pl.multiple_of(j * heads, pair_rows), pair_rows), :] = jnp.where(lane == 0, m, total)
        return 0

    for g in range(GROUPS):
        lax.fori_loop(g * per, (g + 1) * per, attend, 0)
        for a in range(n_sq // block):
            tile = stat[a * dim:(a + 1) * dim, :].T[0:8, :]
            for k in range(block):
                msg[g, a * block + k, rows:rows + 8, :] = tile
    for i in range(chunks):
        wr(i, k_vm, k_out, kosem).wait()
        wr(i, v_vm, v_out, vosem).wait()


def merge_kernel(n_tp, n_sq, heads, msg, wo, y_out, got, fac, att, part, got3,
                 s12, r12, s3, r3, s4a, r4a, s4b, r4b, s4c, r4c):
    dim = msg.shape[-1]
    own, width = part.shape[1:]
    rows = own * heads
    cols = width // n_tp
    n_x = n_sq // 2
    s = lax.axis_index("sq")
    t = lax.axis_index("tp")
    x, c = s // 2, lax.rem(s, 2)

    def sq_peer(i):
        return lax.rem(s + i, n_sq)

    def x_peer(i):
        return lax.rem(x + i, n_x) * 2 + c

    def y_peer(i):
        return lax.rem(t + i, n_tp)

    barrier = pltpu.get_barrier_semaphore()
    for i in range(1, n_sq):
        pl.semaphore_signal(barrier, inc=1, device_id={"sq": sq_peer(i)}, device_id_type=MESH)
    for i in range(1, n_tp):
        pl.semaphore_signal(barrier, inc=1, device_id={"tp": y_peer(i)}, device_id_type=MESH)
    pl.semaphore_wait(barrier, n_sq - 1 + n_tp - 1)

    block = dim // rows

    def copy12(g, i):
        return pltpu.make_async_remote_copy(msg.at[g, sq_peer(i)], got.at[g, i], s12.at[g, i], r12.at[g, i],
                                            device_id={"sq": sq_peer(i)}, device_id_type=MESH)

    def send12(g):
        for i in range(1, n_sq):
            copy12(g, i).start()

    def copy3(g, i):
        span = pl.ds(pl.multiple_of(y_peer(i) * cols, cols), cols)
        return pltpu.make_async_remote_copy(part.at[g, :, span], got3.at[g, i], s3.at[g, i], r3.at[g, i],
                                            device_id={"tp": y_peer(i)}, device_id_type=MESH)

    def proc12(g):
        for i in range(1, n_sq):
            copy12(g, i).wait_recv()
        tiles = [msg[g, s, rows:rows + 8, :]] + [got[g, i, rows:rows + 8, :] for i in range(1, n_sq)]
        m = jnp.concatenate([v[0:1] for v in tiles], axis=0)
        total = jnp.concatenate([v[1:2] for v in tiles], axis=0)
        f = jnp.exp(m - jnp.max(m, axis=0, keepdims=True))
        f = f / jnp.sum(f * total, axis=0, keepdims=True)
        fac[...] = jnp.concatenate([f, jnp.zeros((dim - n_sq, dim), F32)], axis=0).T
        fcol = fac[pl.ds(pl.multiple_of(lax.rem(s, block) * rows, rows), rows), :]
        a = msg[g, s, 0:rows, :] * fcol[:, 0:1]
        for i in range(1, n_sq):
            a = a + got[g, i, 0:rows, :] * fcol[:, i:i + 1]
        att[...] = a
        lhs = jnp.concatenate([att[pl.ds(h, own, stride=heads), :] for h in range(heads)], axis=1).astype(BF16)
        part[g] = jnp.dot(lhs, wo[...], preferred_element_type=F32)
        for i in range(1, n_tp):
            copy3(g, i).start()

    mine = pl.ds(pl.multiple_of(t * cols, cols), cols)

    def copy4a(g, i):
        if g % 2 == 0:
            to = {"sq": x_peer(i)}
        else:
            to = {"tp": y_peer(i)}
        ref = y_out.at[g, x, c, :, mine]
        return pltpu.make_async_remote_copy(ref, ref, s4a.at[g, i], r4a.at[g, i], device_id=to, device_id_type=MESH)

    def from4a(g, i):
        if g % 2 == 0:
            ref = y_out.at[g, lax.rem(x + n_x - i, n_x), c, :, mine]
            to = {"sq": x_peer(i)}
        else:
            src = lax.rem(t + n_tp - i, n_tp)
            ref = y_out.at[g, x, c, :, pl.ds(pl.multiple_of(src * cols, cols), cols)]
            to = {"tp": y_peer(i)}
        return pltpu.make_async_remote_copy(ref, ref, s4a.at[g, i], r4a.at[g, i], device_id=to, device_id_type=MESH)

    def strip(g, i):
        if g % 2 == 0:
            src = lax.rem(t + n_tp - i, n_tp)
            return y_out.at[g, :, c, :, pl.ds(pl.multiple_of(src * cols, cols), cols)]
        return y_out.at[g, lax.rem(x + n_x - i, n_x), c]

    def copy4b(g, i, ref):
        to = {"tp": y_peer(i)} if g % 2 == 0 else {"sq": x_peer(i)}
        return pltpu.make_async_remote_copy(ref, ref, s4b.at[g, i], r4b.at[g, i], device_id=to, device_id_type=MESH)

    def copy4c(g, i):
        ref = strip(g, i)
        return pltpu.make_async_remote_copy(ref, ref, s4c.at[g, i], r4c.at[g, i], device_id={"sq": s + 1 - 2 * c}, device_id_type=MESH)

    def from4c(g, i):
        if g % 2 == 0:
            src = lax.rem(t + n_tp - i, n_tp)
            ref = y_out.at[g, :, 1 - c, :, pl.ds(pl.multiple_of(src * cols, cols), cols)]
        else:
            ref = y_out.at[g, lax.rem(x + n_x - i, n_x), 1 - c]
        return pltpu.make_async_remote_copy(ref, ref, s4c.at[g, i], r4c.at[g, i], device_id={"sq": s + 1 - 2 * c}, device_id_type=MESH)

    def n_a(g):
        return n_x if g % 2 == 0 else n_tp

    def n_b(g):
        return n_tp if g % 2 == 0 else n_x

    def proc3(g):
        for i in range(1, n_tp):
            copy3(g, i).wait_recv()
        y = part[g, :, mine]
        for i in range(1, n_tp):
            y = y + got3[g, i]
        y_out[g, x, c, :, mine] = y
        for i in range(1, n_a(g)):
            copy4a(g, i).start()

    def fwd4(g):
        for i in range(1, n_a(g)):
            from4a(g, i).wait_recv()
        for i in range(1, n_b(g)):
            copy4b(g, i, strip(g, 0)).start()
        copy4c(g, 0).start()

    def end4(g):
        for i in range(1, n_b(g)):
            copy4b(g, i, strip(g, i)).wait_recv()
            copy4c(g, i).start()

    for g in range(GROUPS):
        send12(g)
    for g in range(GROUPS):
        proc12(g)
        if g >= 1:
            proc3(g - 1)
        if g >= 2:
            fwd4(g - 2)
        if g >= 3:
            end4(g - 3)
    proc3(GROUPS - 1)
    for g in range(GROUPS - 2, GROUPS):
        fwd4(g)
        end4(g - 1)
    end4(GROUPS - 1)
    for g in range(GROUPS):
        for i in range(n_b(g)):
            from4c(g, i).wait_recv()
    for g in range(GROUPS):
        for i in range(1, n_sq):
            copy12(g, i).wait_send()
        for i in range(1, n_tp):
            copy3(g, i).wait_send()
        for i in range(1, n_a(g)):
            copy4a(g, i).wait_send()
        for i in range(1, n_b(g)):
            copy4b(g, i, strip(g, 0)).wait_send()
        for i in range(n_b(g)):
            copy4c(g, i).wait_send()


VM = pl.BlockSpec(memory_space=pltpu.VMEM)
SM = pl.BlockSpec(memory_space=pltpu.SMEM)
ANYW = pl.BlockSpec(memory_space=pl.ANY)
DMA = pltpu.SemaphoreType.DMA


def attend(n_sq, cache_lens, hidden, ln_gain, ln_bias, w_query, b_query, w_kv, b_kv, k_cache, v_cache):
    batch, pos, dim = k_cache.shape
    heads = w_query.shape[1] // dim
    chunks = batch // CHUNK
    rows = batch // GROUPS // n_sq * heads
    return pl.pallas_call(
        functools.partial(attend_kernel, n_sq),
        in_specs=[SM, ANYW, VM, VM, ANYW, VM, ANYW, VM, ANYW, ANYW],
        out_specs=[ANYW, ANYW, VM],
        out_shape=[jax.ShapeDtypeStruct(k_cache.shape, BF16), jax.ShapeDtypeStruct(v_cache.shape, BF16),
                   pltpu.VMEM((GROUPS, n_sq, rows + 8, dim), F32)],
        scratch_shapes=[
            pltpu.VMEM(hidden.shape, BF16), pltpu.VMEM(w_query.shape, BF16), pltpu.VMEM(w_kv.shape, BF16),
            pltpu.VMEM(hidden.shape, BF16), pltpu.VMEM((batch, 2 * dim), F32),
            pltpu.VMEM((batch // 2, 2 * heads, 2 * dim), F32),
            pltpu.VMEM((batch // GROUPS * heads, dim), F32),
            pltpu.VMEM(k_cache.shape, BF16), pltpu.VMEM(v_cache.shape, BF16),
            DMA((3,)), *[DMA((chunks,)) for _ in range(4)],
        ],
        compiler_params=pltpu.CompilerParams(vmem_limit_bytes=54 << 20),
        cost_estimate=pl.CostEstimate(flops=4 * batch * pos * dim * heads * 2, bytes_accessed=4 * k_cache.size, transcendentals=0),
        name="attend",
    )(cache_lens, hidden, ln_gain.reshape(1, -1), ln_bias.reshape(1, -1), w_query, b_query.reshape(1, -1),
      w_kv, b_kv.reshape(1, -1), k_cache, v_cache)


def merge(n_tp, n_sq, batch, heads, msg, w_out):
    dim = msg.shape[-1]
    width = w_out.shape[1]
    own = batch // GROUPS // n_sq
    cols = width // n_tp
    sems = [DMA((GROUPS, n)) for n in (n_sq, n_sq, n_tp, n_tp) + (max(n_tp, n_sq // 2),) * 6]
    return pl.pallas_call(
        functools.partial(merge_kernel, n_tp, n_sq, heads),
        in_specs=[VM, VM],
        out_specs=VM,
        out_shape=pltpu.VMEM((GROUPS, n_sq // 2, 2, own, width), F32),
        scratch_shapes=[
            pltpu.VMEM(msg.shape, F32), pltpu.VMEM((dim, dim), F32), pltpu.VMEM((own * heads, dim), F32),
            pltpu.VMEM((GROUPS, own, width), F32), pltpu.VMEM((GROUPS, n_tp, own, cols), F32), *sems,
        ],
        compiler_params=pltpu.CompilerParams(collective_id=0, has_side_effects=True, vmem_limit_bytes=8 << 20),
        cost_estimate=pl.CostEstimate(flops=40 * batch * 256 * dim * heads, bytes_accessed=4 * batch * width, transcendentals=0),
        name="merge",
    )(msg, w_out)


def solution(mesh):
    n_tp, n_sq = mesh.shape["tp"], mesh.shape["sq"]

    def local_step(hidden, cache_lens, k_cache, v_cache, ln_gain, ln_bias, w_query, b_query, w_kv, b_kv, w_out, b_out):
        batch, pos, dim = k_cache.shape
        heads = w_query.shape[1] // dim
        key_new, val_new, msg = attend(n_sq, cache_lens, hidden, ln_gain, ln_bias, w_query, b_query, w_kv, b_kv, k_cache, v_cache)
        y = merge(n_tp, n_sq, batch, heads, msg, w_out)
        out_hidden = (hidden.astype(F32) + y.reshape(hidden.shape) + b_out).astype(BF16)
        return out_hidden, key_new, val_new

    cache_spec = P("dp", "sq", None)
    row_spec = P("dp", None)
    in_specs = (row_spec, P("dp"), cache_spec, cache_spec, P(None), P(None), P(None, "tp"), P("tp"), P(None, None), P(None), P("tp", None), P(None))
    return jax.shard_map(local_step, mesh=mesh, in_specs=in_specs, out_specs=(row_spec, cache_spec, cache_spec), check_vma=False)
```

time: 194 us -> 66.2 us (0.34)
  waiting for transfers between devices: 96.4 us -> 0 us
  blocking collectives: 45.7 us -> 0 us
  Pallas kernels: 28 us -> 64.1 us
  between operations: 14.1 us -> 0.7 us
  other arithmetic: 6.81 us -> 1.29 us
  matrix products: 2.01 us -> 0 us
    psum x2 -> x0, waiting for transfers between devices: 96.3 us -> none  [the longest x1 54.6 us: local_step(): projected = lax.psum(jnp.dot(att, w_out, preferred_element_type=F32), 'tp')]
    pallas_call x1 -> x2, Pallas kernels: 28 us -> 64.1 us  [the longest x1 36.5 us: merge(): pl.pallas_call(functools.partial(merge_kernel, n_tp, n_sq, heads), in_spe...]
    pmax x1 -> x0, blocking collectives: 30 us -> none  [local_step(): top = lax.pmax(m, 'sq')]
    psum x1 -> x0, blocking collectives: 15.7 us -> none  [local_step(): den = lax.psum(total * f, 'sq')]
    convert_element_type x2 -> x1, other arithmetic: 4.12 us -> 1.29 us  [local_step(): (hidden.astype(F32) + y.reshape(hidden.shape) + b_out).astype(BF16)]
    mul x2 -> x0, other arithmetic: 2.69 us -> none  [the longest x1 1.7 us: local_step(): den = lax.psum(total * f, 'sq')]
    dot_general x1 -> x0, matrix products: 2.01 us -> none  [local_step(): projected = lax.psum(jnp.dot(att, w_out, preferred_element_type=F32), 'tp')]
  transfers between devices with their start and end apart: 2 -> 0, of which waited for: 2 -> 0; matrix products, arithmetic and copies ran while one was open for 0% -> 0% of each run, Pallas kernels for 0% -> 0%
where the time goes in v2:
time: 66.2 us; the launch traced here: 66.1 us
  Pallas kernels  64.1 us (97%)
  other arithmetic  1.29 us (2%)
  between operations  0.7 us (1%)
    pallas_call x1, Pallas kernels, merge(): pl.pallas_call(functools.partial(merge_kernel, n_tp, n_sq, heads), in_spe...  36.5 us
    pallas_call x1, Pallas kernels, attend(): pl.pallas_call(functools.partial(attend_kernel, n_sq), in_specs=[SM, ANYW...  27.6 us

profile of v2, /device:TPU:97, one launch (start us, length us, event | category | flops | bytes accessed | tf_op | source)
XLA Modules:
  0.0 66.1 jit_solution(15839777160851236908)
XLA Ops:
  0.6 0.0 copy-start
  0.6 27.6 %attend.1 = (bf16[256,256,128]{2,1,0:T(8,128)(2,1)}, bf16[256,256,128]{2,1,0:T(8,128)(2,1)}, f32[4,8,40,128]{3,2,1,0:T(8,128)S(1)}) custom-call(s32[256]{0:T(256)} %lens.1, bf16[256,2048]{1,0:T(8,128)(2,1)} %hid_h.1, f32[1,2048]{1,0:T(1,128)} %bitcast.10, f32[1,2048]{1,0:T(1,128)} %bitcast.11, bf16[2048,512]{1,0:T(8,128)(2,1)} %wq_h.1, f32[1,512]{1,0:T(1,128)} %bitcast.12, ...), custom_call_target="tpu_custom_call" | custom-call | flops 268435456 | bytes 33554432 | tf_op jit(solution)/shard_map/attend/pallas_call | solution.py:310
  28.2 0.0 copy-done
  28.2 0.0 copy-start.1
  28.3 0.0 copy-start.2
  28.3 36.5 %merge.1 = f32[4,4,2,8,2048]{4,3,2,1,0:T(8,128)S(1)} custom-call(f32[4,8,40,128]{3,2,1,0:T(8,128)S(1)} %get-tuple-element.6.msg, bf16[512,2048]{1,0:T(8,128)(2,1)S(1)} %copy-done), custom_call_target="tpu_custom_call" | custom-call | flops 1342177280 | bytes 2097152 | tf_op jit(solution)/shard_map/merge/pallas_call | solution.py:337
  64.8 0.0 copy-done.1
  64.8 0.0 copy-done.2
  64.8 1.3 %fusion.1 = bf16[256,2048]{1,0:T(8,128)(2,1)} fusion(f32[4,4,2,8,2048]{4,3,2,1,0:T(8,128)S(1)} %merge.1, bf16[256,2048]{1,0:T(8,128)(2,1)S(1)} %copy-done.1, f32[2048]{0:T(1024)S(1)} %copy-done.2), kind=kLoop, calls=%fused_computation.2 | loop fusion | flops 2097152 | bytes 4202496 | tf_op jit(solution)/shard_map/convert_element_type | solution.py:360
Async XLA Ops:
  0.6 27.6 %copy-start = (bf16[512,2048]{1,0:T(8,128)(2,1)S(1)}, bf16[512,2048]{1,0:T(8,128)(2,1)}, u32[]{:S(2)}) copy-start(bf16[512,2048]{1,0:T(8,128)(2,1)} %wo.1) | copy-start | bytes 6291460
  28.2 36.6 %copy-start.1 = (bf16[256,2048]{1,0:T(8,128)(2,1)S(1)}, bf16[256,2048]{1,0:T(8,128)(2,1)}, u32[]{:S(2)}) copy-start(bf16[256,2048]{1,0:T(8,128)(2,1)} %hid_h.1) | copy-start | bytes 3145732
  28.3 36.6 %copy-start.2 = (f32[2048]{0:T(1024)S(1)}, f32[2048]{0:T(1024)}, u32[]{:S(2)}) copy-start(f32[2048]{0:T(1024)} %param.23) | copy-start | bytes 24580

commit v3 on v2

--- a/solution.py
+++ b/solution.py
@@ -10,7 +10,8 @@
 BF16 = jnp.bfloat16
 MESH = pl.DeviceIdType.MESH
 CHUNK = 16
-GROUPS = 4
+DEPTH = 5
+GROUPS = 2
 LOW = -1e30
 
 
@@ -38,7 +39,7 @@
 
     for copy in wcopies:
         copy.start()
-    for i in range(chunks):
+    for i in range(DEPTH):
         rd(i, k_in, k_vm, ksem).start()
         rd(i, v_in, v_vm, vsem).start()
 
@@ -82,6 +83,12 @@
     def attend(i, _):
         rd(i, k_in, k_vm, ksem).wait()
         rd(i, v_in, v_vm, vsem).wait()
+
+        @pl.when(i + DEPTH < chunks)
+        def _():
+            rd(i + DEPTH, k_in, k_vm, ksem).start()
+            rd(i + DEPTH, v_in, v_vm, vsem).start()
+
         base = i * CHUNK
         grp = i // per
         tiles = []
@@ -134,166 +141,165 @@
         wr(i, v_vm, v_out, vosem).wait()
 
 
-def merge_kernel(n_tp, n_sq, heads, msg, wo, y_out, got, fac, att, part, got3,
-                 s12, r12, s3, r3, s4a, r4a, s4b, r4b, s4c, r4c):
+def merge_kernel(n_tp, n_sq, heads, msg, wo, y_out, got1, mid, got2, fac, att, part, got3,
+                 s1, r1, s2, r2, s3, r3, s4a, r4a, s4b, r4b, s4c, r4c):
     dim = msg.shape[-1]
     own, width = part.shape[1:]
     rows = own * heads
     cols = width // n_tp
     n_x = n_sq // 2
+    block = dim // rows
     s = lax.axis_index("sq")
     t = lax.axis_index("tp")
     x, c = s // 2, lax.rem(s, 2)
-
-    def sq_peer(i):
-        return lax.rem(s + i, n_sq)
+    partner = {"sq": s + 1 - 2 * c}
 
     def x_peer(i):
-        return lax.rem(x + i, n_x) * 2 + c
+        return {"sq": lax.rem(x + i, n_x) * 2 + c}
 
     def y_peer(i):
-        return lax.rem(t + i, n_tp)
+        return {"tp": lax.rem(t + i, n_tp)}
+
+    def remote(src, dst, send, recv, to):
+        return pltpu.make_async_remote_copy(src, dst, send, recv, device_id=to, device_id_type=MESH)
+
+    def lanes(k, n):
+        return pl.ds(pl.multiple_of(k * n, n), n)
 
     barrier = pltpu.get_barrier_semaphore()
-    for i in range(1, n_sq):
-        pl.semaphore_signal(barrier, inc=1, device_id={"sq": sq_peer(i)}, device_id_type=MESH)
+    pl.semaphore_signal(barrier, inc=1, device_id=partner, device_id_type=MESH)
+    for i in range(1, n_x):
+        pl.semaphore_signal(barrier, inc=1, device_id=x_peer(i), device_id_type=MESH)
     for i in range(1, n_tp):
-        pl.semaphore_signal(barrier, inc=1, device_id={"tp": y_peer(i)}, device_id_type=MESH)
-    pl.semaphore_wait(barrier, n_sq - 1 + n_tp - 1)
-
-    block = dim // rows
-
-    def copy12(g, i):
-        return pltpu.make_async_remote_copy(msg.at[g, sq_peer(i)], got.at[g, i], s12.at[g, i], r12.at[g, i],
-                                            device_id={"sq": sq_peer(i)}, device_id_type=MESH)
-
-    def send12(g):
-        for i in range(1, n_sq):
-            copy12(g, i).start()
+        pl.semaphore_signal(barrier, inc=1, device_id=y_peer(i), device_id_type=MESH)
+    pl.semaphore_wait(barrier, n_x + n_tp - 1)
+
+    def copy1(g):
+        return remote(msg.at[g, :, 1 - c], got1.at[g], s1.at[g], r1.at[g], partner)
+
+    def copy2(g, i):
+        return remote(mid.at[g, lax.rem(x + i, n_x)], got2.at[g, i], s2.at[g, i], r2.at[g, i], x_peer(i))
 
     def copy3(g, i):
-        span = pl.ds(pl.multiple_of(y_peer(i) * cols, cols), cols)
-        return pltpu.make_async_remote_copy(part.at[g, :, span], got3.at[g, i], s3.at[g, i], r3.at[g, i],
-                                            device_id={"tp": y_peer(i)}, device_id_type=MESH)
-
-    def proc12(g):
-        for i in range(1, n_sq):
-            copy12(g, i).wait_recv()
-        tiles = [msg[g, s, rows:rows + 8, :]] + [got[g, i, rows:rows + 8, :] for i in range(1, n_sq)]
+        return remote(part.at[g, :, lanes(lax.rem(t + i, n_tp), cols)], got3.at[g, i], s3.at[g, i], r3.at[g, i], y_peer(i))
+
+    def dims(g):
+        return (n_x, n_tp) if g % 2 == 0 else (n_tp, n_x)
+
+    def peer(g, second, i):
+        return y_peer(i) if (g % 2 == 0) == second else x_peer(i)
+
+    def cell(g, a, b):
+        dx, dt = (a, b) if g % 2 == 0 else (b, a)
+        return y_out.at[g, lax.rem(x + n_x - dx, n_x), c, :, lanes(lax.rem(t + n_tp - dt, n_tp), cols)]
+
+    def copy4a(g, i, back=0):
+        return remote(cell(g, back, 0), cell(g, back, 0), s4a.at[g, i], r4a.at[g, i], peer(g, False, i))
+
+    def copy4b(g, a, i, back=0):
+        return remote(cell(g, a, back), cell(g, a, back), s4b.at[g, a, i], r4b.at[g, a, i], peer(g, True, i))
+
+    def copy4c(g, i, core):
+        if g % 2 == 0:
+            ref = y_out.at[g, :, core, :, lanes(lax.rem(t + n_tp - i, n_tp), cols)]
+        else:
+            ref = y_out.at[g, lax.rem(x + n_x - i, n_x), core]
+        return remote(ref, ref, s4c.at[g, i], r4c.at[g, i], partner)
+
+    def merge1(g):
+        copy1(g).wait_recv()
+        fs, tiles = [], []
+        for k in range(n_x):
+            a, b = msg[g, k, c, rows:rows + 8, :], got1[g, k, rows:rows + 8, :]
+            top = jnp.maximum(a[0:1], b[0:1])
+            fa, fb = jnp.exp(a[0:1] - top), jnp.exp(b[0:1] - top)
+            fs += [fa, fb]
+            mid[g, k, rows:rows + 8, :] = jnp.concatenate([top, fa * a[1:2] + fb * b[1:2], jnp.zeros((6, dim), F32)], axis=0)
+        f = jnp.concatenate(fs + [jnp.zeros((dim - 2 * n_x, dim), F32)], axis=0)
+        fac[...] = f.T
+        for k in range(n_x):
+            fcol = fac[lanes(lax.rem(2 * k + c, block), rows), :]
+            mid[g, k, 0:rows, :] = msg[g, k, c, 0:rows, :] * fcol[:, 2 * k:2 * k + 1] + got1[g, k, 0:rows, :] * fcol[:, 2 * k + 1:2 * k + 2]
+        for i in range(1, n_x):
+            copy2(g, i).start()
+
+    def merge2(g):
+        for i in range(1, n_x):
+            copy2(g, i).wait_recv()
+        tiles = [mid[g, x, rows:rows + 8, :]] + [got2[g, i, rows:rows + 8, :] for i in range(1, n_x)]
         m = jnp.concatenate([v[0:1] for v in tiles], axis=0)
         total = jnp.concatenate([v[1:2] for v in tiles], axis=0)
         f = jnp.exp(m - jnp.max(m, axis=0, keepdims=True))
         f = f / jnp.sum(f * total, axis=0, keepdims=True)
-        fac[...] = jnp.concatenate([f, jnp.zeros((dim - n_sq, dim), F32)], axis=0).T
-        fcol = fac[pl.ds(pl.multiple_of(lax.rem(s, block) * rows, rows), rows), :]
-        a = msg[g, s, 0:rows, :] * fcol[:, 0:1]
-        for i in range(1, n_sq):
-            a = a + got[g, i, 0:rows, :] * fcol[:, i:i + 1]
+        fac[...] = jnp.concatenate([f, jnp.zeros((dim - n_x, dim), F32)], axis=0).T
+        fcol = fac[lanes(lax.rem(s, block), rows), :]
+        a = mid[g, x, 0:rows, :] * fcol[:, 0:1]
+        for i in range(1, n_x):
+            a = a + got2[g, i, 0:rows, :] * fcol[:, i:i + 1]
         att[...] = a
         lhs = jnp.concatenate([att[pl.ds(h, own, stride=heads), :] for h in range(heads)], axis=1).astype(BF16)
         part[g] = jnp.dot(lhs, wo[...], preferred_element_type=F32)
         for i in range(1, n_tp):
             copy3(g, i).start()
 
-    mine = pl.ds(pl.multiple_of(t * cols, cols), cols)
-
-    def copy4a(g, i):
-        if g % 2 == 0:
-            to = {"sq": x_peer(i)}
-        else:
-            to = {"tp": y_peer(i)}
-        ref = y_out.at[g, x, c, :, mine]
-        return pltpu.make_async_remote_copy(ref, ref, s4a.at[g, i], r4a.at[g, i], device_id=to, device_id_type=MESH)
-
-    def from4a(g, i):
-        if g % 2 == 0:
-            ref = y_out.at[g, lax.rem(x + n_x - i, n_x), c, :, mine]
-            to = {"sq": x_peer(i)}
-        else:
-            src = lax.rem(t + n_tp - i, n_tp)
-            ref = y_out.at[g, x, c, :, pl.ds(pl.multiple_of(src * cols, cols), cols)]
-            to = {"tp": y_peer(i)}
-        return pltpu.make_async_remote_copy(ref, ref, s4a.at[g, i], r4a.at[g, i], device_id=to, device_id_type=MESH)
-
-    def strip(g, i):
-        if g % 2 == 0:
-            src = lax.rem(t + n_tp - i, n_tp)
-            return y_out.at[g, :, c, :, pl.ds(pl.multiple_of(src * cols, cols), cols)]
-        return y_out.at[g, lax.rem(x + n_x - i, n_x), c]
-
-    def copy4b(g, i, ref):
-        to = {"tp": y_peer(i)} if g % 2 == 0 else {"sq": x_peer(i)}
-        return pltpu.make_async_remote_copy(ref, ref, s4b.at[g, i], r4b.at[g, i], device_id=to, device_id_type=MESH)
-
-    def copy4c(g, i):
-        ref = strip(g, i)
-        return pltpu.make_async_remote_copy(ref, ref, s4c.at[g, i], r4c.at[g, i], device_id={"sq": s + 1 - 2 * c}, device_id_type=MESH)
-
-    def from4c(g, i):
-        if g % 2 == 0:
-            src = lax.rem(t + n_tp - i, n_tp)
-            ref = y_out.at[g, :, 1 - c, :, pl.ds(pl.multiple_of(src * cols, cols), cols)]
-        else:
-            ref = y_out.at[g, lax.rem(x + n_x - i, n_x), 1 - c]
-        return pltpu.make_async_remote_copy(ref, ref, s4c.at[g, i], r4c.at[g, i], device_id={"sq": s + 1 - 2 * c}, device_id_type=MESH)
-
-    def n_a(g):
-        return n_x if g % 2 == 0 else n_tp
-
-    def n_b(g):
-        return n_tp if g % 2 == 0 else n_x
-
-    def proc3(g):
+    def reduce3(g):
         for i in range(1, n_tp):
             copy3(g, i).wait_recv()
-        y = part[g, :, mine]
+        y = part[g, :, lanes(t, cols)]
         for i in range(1, n_tp):
             y = y + got3[g, i]
-        y_out[g, x, c, :, mine] = y
-        for i in range(1, n_a(g)):
+        y_out[g, x, c, :, lanes(t, cols)] = y
+        na, nb = dims(g)
+        for i in range(1, na):
             copy4a(g, i).start()
-
-    def fwd4(g):
-        for i in range(1, n_a(g)):
-            from4a(g, i).wait_recv()
-        for i in range(1, n_b(g)):
-            copy4b(g, i, strip(g, 0)).start()
-        copy4c(g, 0).start()
-
-    def end4(g):
-        for i in range(1, n_b(g)):
-            copy4b(g, i, strip(g, i)).wait_recv()
-            copy4c(g, i).start()
-
-    for g in range(GROUPS):
-        send12(g)
-    for g in range(GROUPS):
-        proc12(g)
-        if g >= 1:
-            proc3(g - 1)
-        if g >= 2:
-            fwd4(g - 2)
-        if g >= 3:
-            end4(g - 3)
-    proc3(GROUPS - 1)
-    for g in range(GROUPS - 2, GROUPS):
-        fwd4(g)
-        end4(g - 1)
-    end4(GROUPS - 1)
-    for g in range(GROUPS):
-        for i in range(n_b(g)):
-            from4c(g, i).wait_recv()
-    for g in range(GROUPS):
-        for i in range(1, n_sq):
-            copy12(g, i).wait_send()
+        for i in range(1, nb):
+            copy4b(g, 0, i).start()
+
+    def nearest(n):
+        return sorted(range(1, n), key=lambda i: min(i, n - i))
+
+    def forward4(g):
+        na, nb = dims(g)
+        for a in nearest(na):
+            copy4a(g, a, a).wait_recv()
+            for i in range(1, nb):
+                copy4b(g, a, i).start()
+        copy4c(g, 0, c).start()
+
+    def collect4(g):
+        na, nb = dims(g)
+        for i in nearest(nb):
+            for a in range(na):
+                copy4b(g, a, i, i).wait_recv()
+            copy4c(g, i, c).start()
+
+    for g in range(GROUPS):
+        copy1(g).start()
+    for g in range(GROUPS):
+        merge1(g)
+    stages = (merge2, reduce3, forward4, collect4)
+    for step in range(GROUPS + len(stages) - 1):
+        for k, stage in enumerate(stages):
+            if 0 <= step - k < GROUPS:
+                stage(step - k)
+    for g in range(GROUPS):
+        na, nb = dims(g)
+        for i in range(nb):
+            copy4c(g, i, 1 - c).wait_recv()
+    for g in range(GROUPS):
+        na, nb = dims(g)
+        copy1(g).wait_send()
+        for i in range(1, n_x):
+            copy2(g, i).wait_send()
         for i in range(1, n_tp):
             copy3(g, i).wait_send()
-        for i in range(1, n_a(g)):
+        for i in range(1, na):
             copy4a(g, i).wait_send()
-        for i in range(1, n_b(g)):
-            copy4b(g, i, strip(g, 0)).wait_send()
-        for i in range(n_b(g)):
-            copy4c(g, i).wait_send()
+        for a in range(na):
+            for i in range(1, nb):
+                copy4b(g, a, i).wait_send()
+        for i in range(nb):
+            copy4c(g, i, c).wait_send()
 
 
 VM = pl.BlockSpec(memory_space=pltpu.VMEM)
@@ -333,20 +339,24 @@
     width = w_out.shape[1]
     own = batch // GROUPS // n_sq
     cols = width // n_tp
-    sems = [DMA((GROUPS, n)) for n in (n_sq, n_sq, n_tp, n_tp) + (max(n_tp, n_sq // 2),) * 6]
+    n_x = n_sq // 2
+    most = max(n_tp, n_x)
+    shapes = [(GROUPS,), (GROUPS, n_x), (GROUPS, n_tp), (GROUPS, most), (GROUPS, most, most), (GROUPS, most)]
     return pl.pallas_call(
         functools.partial(merge_kernel, n_tp, n_sq, heads),
         in_specs=[VM, VM],
         out_specs=VM,
-        out_shape=pltpu.VMEM((GROUPS, n_sq // 2, 2, own, width), F32),
+        out_shape=pltpu.VMEM((GROUPS, n_x, 2, own, width), F32),
         scratch_shapes=[
-            pltpu.VMEM(msg.shape, F32), pltpu.VMEM((dim, dim), F32), pltpu.VMEM((own * heads, dim), F32),
-            pltpu.VMEM((GROUPS, own, width), F32), pltpu.VMEM((GROUPS, n_tp, own, cols), F32), *sems,
+            *[pltpu.VMEM((GROUPS, n_x, *msg.shape[2:]), F32) for _ in range(3)],
+            pltpu.VMEM((dim, dim), F32), pltpu.VMEM((own * heads, dim), F32),
+            pltpu.VMEM((GROUPS, own, width), F32), pltpu.VMEM((GROUPS, n_tp, own, cols), F32),
+            *[DMA(shape) for shape in shapes for _ in range(2)],
         ],
         compiler_params=pltpu.CompilerParams(collective_id=0, has_side_effects=True, vmem_limit_bytes=8 << 20),
         cost_estimate=pl.CostEstimate(flops=40 * batch * 256 * dim * heads, bytes_accessed=4 * batch * width, transcendentals=0),
         name="merge",
-    )(msg, w_out)
+    )(msg.reshape(GROUPS, n_x, 2, *msg.shape[2:]), w_out)
 
 
 def solution(mesh):

time: 66.2 us -> 61.7 us (0.932)
  Pallas kernels: 64.1 us -> 59.6 us
    pallas_call x1, Pallas kernels: 36.5 us -> 31.6 us  [merge(): pl.pallas_call(functools.partial(merge_kernel, n_tp, n_sq, heads), in_spe...]
where the time goes in v3:
time: 61.7 us; the launch traced here: 61.6 us
  Pallas kernels  59.6 us (97%)
  other arithmetic  1.29 us (2%)
  between operations  0.7 us (1%)
    pallas_call x1, Pallas kernels, merge(): pl.pallas_call(functools.partial(merge_kernel, n_tp, n_sq, heads), in_spe...  31.6 us
    pallas_call x1, Pallas kernels, attend(): pl.pallas_call(functools.partial(attend_kernel, n_sq), in_specs=[SM, ANYW...  27.9 us
    convert_element_type x1, other arithmetic, local_step(): (hidden.astype(F32) + y.reshape(hidden.shape) + b_out).astype(BF16)  1.29 us

profile of v3, /device:TPU:97, one launch (start us, length us, event | category | flops | bytes accessed | tf_op | source)
XLA Modules:
  0.0 61.6 jit_solution(13806363596484770864)
XLA Ops:
  0.6 0.0 copy-start
  0.6 27.9 %attend.1 = (bf16[256,256,128]{2,1,0:T(8,128)(2,1)}, bf16[256,256,128]{2,1,0:T(8,128)(2,1)}, f32[2,8,72,128]{3,2,1,0:T(8,128)S(1)}) custom-call(s32[256]{0:T(256)} %lens.1, bf16[256,2048]{1,0:T(8,128)(2,1)} %hid_h.1, f32[1,2048]{1,0:T(1,128)} %bitcast.12, f32[1,2048]{1,0:T(1,128)} %bitcast.13, bf16[2048,512]{1,0:T(8,128)(2,1)} %wq_h.1, f32[1,512]{1,0:T(1,128)} %bitcast.14, ...), custom_call_target="tpu_custom_call" | custom-call | flops 268435456 | bytes 33554432 | tf_op jit(solution)/shard_map/attend/pallas_call | solution.py:316
  28.6 0.0 copy-done
  28.6 0.0 copy-start.1
  28.6 0.0 copy-start.2
  28.6 31.6 %merge.1 = f32[2,4,2,16,2048]{4,3,2,1,0:T(8,128)S(1)} custom-call(f32[2,4,2,72,128]{4,3,2,1,0:T(8,128)S(1)} %bitcast.11, bf16[512,2048]{1,0:T(8,128)(2,1)S(1)} %copy-done), custom_call_target="tpu_custom_call" | custom-call | flops 1342177280 | bytes 2097152 | tf_op jit(solution)/shard_map/merge/pallas_call | solution.py:345
  60.3 0.0 copy-done.1
  60.3 0.0 copy-done.2
  60.3 1.3 %fusion.1 = bf16[256,2048]{1,0:T(8,128)(2,1)} fusion(f32[2,4,2,16,2048]{4,3,2,1,0:T(8,128)S(1)} %merge.1, bf16[256,2048]{1,0:T(8,128)(2,1)S(1)} %copy-done.1, f32[2048]{0:T(1024)S(1)} %copy-done.2), kind=kLoop, calls=%fused_computation.2 | loop fusion | flops 2097152 | bytes 4202496 | tf_op jit(solution)/shard_map/convert_element_type | solution.py:370
Async XLA Ops:
  0.6 27.9 %copy-start = (bf16[512,2048]{1,0:T(8,128)(2,1)S(1)}, bf16[512,2048]{1,0:T(8,128)(2,1)}, u32[]{:S(2)}) copy-start(bf16[512,2048]{1,0:T(8,128)(2,1)} %wo.1) | copy-start | bytes 6291460
  28.6 31.7 %copy-start.1 = (bf16[256,2048]{1,0:T(8,128)(2,1)S(1)}, bf16[256,2048]{1,0:T(8,128)(2,1)}, u32[]{:S(2)}) copy-start(bf16[256,2048]{1,0:T(8,128)(2,1)} %hid_h.1) | copy-start | bytes 3145732
  28.6 31.7 %copy-start.2 = (f32[2048]{0:T(1024)S(1)}, f32[2048]{0:T(1024)}, u32[]{:S(2)}) copy-start(f32[2048]{0:T(1024)} %param.23) | copy-start | bytes 24580

commit v4 on v3

--- a/solution.py
+++ b/solution.py
@@ -10,7 +10,8 @@
 BF16 = jnp.bfloat16
 MESH = pl.DeviceIdType.MESH
 CHUNK = 16
-DEPTH = 5
+DEPTH = 8
+EARLY = 3
 GROUPS = 2
 LOW = -1e30
 
@@ -39,11 +40,11 @@
 
     for copy in wcopies:
         copy.start()
-    for i in range(DEPTH):
+
+    wcopies[0].wait()
+    for i in range(EARLY):
         rd(i, k_in, k_vm, ksem).start()
         rd(i, v_in, v_vm, vsem).start()
-
-    wcopies[0].wait()
     nrow = 32
 
     def norm_rows(i, _):
@@ -58,9 +59,12 @@
 
     lax.fori_loop(0, batch // nrow, norm_rows, 0)
     wcopies[1].wait()
+    wcopies[2].wait()
+    for i in range(EARLY, DEPTH):
+        rd(i, k_in, k_vm, ksem).start()
+        rd(i, v_in, v_vm, vsem).start()
     kv = jnp.dot(h_scr[...], wkv[...], preferred_element_type=F32) + bkv[...]
     kv_scr[...] = kv.astype(BF16).astype(F32)
-    wcopies[2].wait()
     qd[...] = jnp.zeros_like(qd)
     for h in range(heads):
         span = slice(h * dim, (h + 1) * dim)

time: 61.7 us -> 58.9 us (0.955)
  Pallas kernels: 59.6 us -> 56.8 us
    pallas_call x1, Pallas kernels: 27.9 us -> 25.2 us  [attend(): pl.pallas_call(functools.partial(attend_kernel, n_sq), in_specs=[SM, ANYW...]
where the time goes in v4:
time: 58.9 us; the launch traced here: 58.8 us
  Pallas kernels  56.8 us (96%)
  other arithmetic  1.29 us (2%)
  between operations  0.7 us (1%)
    pallas_call x1, Pallas kernels, merge(): pl.pallas_call(functools.partial(merge_kernel, n_tp, n_sq, heads), in_spe...  31.6 us
    pallas_call x1, Pallas kernels, attend(): pl.pallas_call(functools.partial(attend_kernel, n_sq), in_specs=[SM, ANYW...  25.2 us
    convert_element_type x1, other arithmetic, local_step(): (hidden.astype(F32) + y.reshape(hidden.shape) + b_out).astype(BF16)  1.29 us

profile of v4, /device:TPU:97, one launch (start us, length us, event | category | flops | bytes accessed | tf_op | source)
XLA Modules:
  0.0 58.8 jit_solution(10336730578384666043)
XLA Ops:
  0.6 0.0 copy-start
  0.6 25.2 %attend.1 = (bf16[256,256,128]{2,1,0:T(8,128)(2,1)}, bf16[256,256,128]{2,1,0:T(8,128)(2,1)}, f32[2,8,72,128]{3,2,1,0:T(8,128)S(1)}) custom-call(s32[256]{0:T(256)} %lens.1, bf16[256,2048]{1,0:T(8,128)(2,1)} %hid_h.1, f32[1,2048]{1,0:T(1,128)} %bitcast.12, f32[1,2048]{1,0:T(1,128)} %bitcast.13, bf16[2048,512]{1,0:T(8,128)(2,1)} %wq_h.1, f32[1,512]{1,0:T(1,128)} %bitcast.14, ...), custom_call_target="tpu_custom_call" | custom-call | flops 268435456 | bytes 33554432 | tf_op jit(solution)/shard_map/attend/pallas_call | solution.py:320
  25.9 0.0 copy-done
  25.9 0.0 copy-start.1
  25.9 0.0 copy-start.2
  25.9 31.6 %merge.1 = f32[2,4,2,16,2048]{4,3,2,1,0:T(8,128)S(1)} custom-call(f32[2,4,2,72,128]{4,3,2,1,0:T(8,128)S(1)} %bitcast.11, bf16[512,2048]{1,0:T(8,128)(2,1)S(1)} %copy-done), custom_call_target="tpu_custom_call" | custom-call | flops 1342177280 | bytes 2097152 | tf_op jit(solution)/shard_map/merge/pallas_call | solution.py:349
  57.5 0.0 copy-done.1
  57.5 0.0 copy-done.2
  57.6 1.3 %fusion.1 = bf16[256,2048]{1,0:T(8,128)(2,1)} fusion(f32[2,4,2,16,2048]{4,3,2,1,0:T(8,128)S(1)} %merge.1, bf16[256,2048]{1,0:T(8,128)(2,1)S(1)} %copy-done.1, f32[2048]{0:T(1024)S(1)} %copy-done.2), kind=kLoop, calls=%fused_computation.2 | loop fusion | flops 2097152 | bytes 4202496 | tf_op jit(solution)/shard_map/convert_element_type | solution.py:374
Async XLA Ops:
  0.6 25.2 %copy-start = (bf16[512,2048]{1,0:T(8,128)(2,1)S(1)}, bf16[512,2048]{1,0:T(8,128)(2,1)}, u32[]{:S(2)}) copy-start(bf16[512,2048]{1,0:T(8,128)(2,1)} %wo.1) | copy-start | bytes 6291460
  25.9 31.7 %copy-start.1 = (bf16[256,2048]{1,0:T(8,128)(2,1)S(1)}, bf16[256,2048]{1,0:T(8,128)(2,1)}, u32[]{:S(2)}) copy-start(bf16[256,2048]{1,0:T(8,128)(2,1)} %hid_h.1) | copy-start | bytes 3145732
  25.9 31.7 %copy-start.2 = (f32[2048]{0:T(1024)S(1)}, f32[2048]{0:T(1024)}, u32[]{:S(2)}) copy-start(f32[2048]{0:T(1024)} %param.23) | copy-start | bytes 24580

commit v5 on v4

--- a/solution.py
+++ b/solution.py
@@ -13,7 +13,7 @@
 DEPTH = 8
 EARLY = 3
 GROUPS = 2
-LOW = -1e30
+LOW = float(jnp.finfo(F32).min)
 
 
 def attend_kernel(n_sq, lens, hid_h, gain, bias, wq_h, bq, wkv_h, bkv, k_in, v_in,
@@ -188,13 +188,13 @@
         return remote(part.at[g, :, lanes(lax.rem(t + i, n_tp), cols)], got3.at[g, i], s3.at[g, i], r3.at[g, i], y_peer(i))
 
     def dims(g):
-        return (n_x, n_tp) if g % 2 == 0 else (n_tp, n_x)
+        return (n_x, n_tp) if g % 2 == 1 else (n_tp, n_x)
 
     def peer(g, second, i):
-        return y_peer(i) if (g % 2 == 0) == second else x_peer(i)
+        return y_peer(i) if (g % 2 == 1) == second else x_peer(i)
 
     def cell(g, a, b):
-        dx, dt = (a, b) if g % 2 == 0 else (b, a)
+        dx, dt = (a, b) if g % 2 == 1 else (b, a)
         return y_out.at[g, lax.rem(x + n_x - dx, n_x), c, :, lanes(lax.rem(t + n_tp - dt, n_tp), cols)]
 
     def copy4a(g, i, back=0):
@@ -204,7 +204,7 @@
         return remote(cell(g, a, back), cell(g, a, back), s4b.at[g, a, i], r4b.at[g, a, i], peer(g, True, i))
 
     def copy4c(g, i, core):
-        if g % 2 == 0:
+        if g % 2 == 1:
             ref = y_out.at[g, :, core, :, lanes(lax.rem(t + n_tp - i, n_tp), cols)]
         else:
             ref = y_out.at[g, lax.rem(x + n_x - i, n_x), core]

time: 58.9 us -> 59.1 us (level)
  no operation moved by 1% of the time
where the time goes in v5:
time: 59.1 us
  Pallas kernels  57.1 us (97%)
  other arithmetic  1.29 us (2%)
  between operations  0.7 us (1%)
    pallas_call x1, Pallas kernels, merge(): pl.pallas_call(functools.partial(merge_kernel, n_tp, n_sq, heads), in_spe...  31.9 us
    pallas_call x1, Pallas kernels, attend(): pl.pallas_call(functools.partial(attend_kernel, n_sq), in_specs=[SM, ANYW...  25.2 us
    convert_element_type x1, other arithmetic, local_step(): (hidden.astype(F32) + y.reshape(hidden.shape) + b_out).astype(BF16)  1.29 us

profile of v5, /device:TPU:97, one launch (start us, length us, event | category | flops | bytes accessed | tf_op | source)
XLA Modules:
  0.0 59.1 jit_solution(1227269704681224995)
XLA Ops:
  0.6 0.0 copy-start
  0.6 25.2 %attend.1 = (bf16[256,256,128]{2,1,0:T(8,128)(2,1)}, bf16[256,256,128]{2,1,0:T(8,128)(2,1)}, f32[2,8,72,128]{3,2,1,0:T(8,128)S(1)}) custom-call(s32[256]{0:T(256)} %lens.1, bf16[256,2048]{1,0:T(8,128)(2,1)} %hid_h.1, f32[1,2048]{1,0:T(1,128)} %bitcast.12, f32[1,2048]{1,0:T(1,128)} %bitcast.13, bf16[2048,512]{1,0:T(8,128)(2,1)} %wq_h.1, f32[1,512]{1,0:T(1,128)} %bitcast.14, ...), custom_call_target="tpu_custom_call" | custom-call | flops 268435456 | bytes 33554432 | tf_op jit(solution)/shard_map/attend/pallas_call | solution.py:320
  25.9 0.0 copy-done
  25.9 0.0 copy-start.1
  25.9 0.0 copy-start.2
  25.9 31.9 %merge.1 = f32[2,4,2,16,2048]{4,3,2,1,0:T(8,128)S(1)} custom-call(f32[2,4,2,72,128]{4,3,2,1,0:T(8,128)S(1)} %bitcast.11, bf16[512,2048]{1,0:T(8,128)(2,1)S(1)} %copy-done), custom_call_target="tpu_custom_call" | custom-call | flops 1342177280 | bytes 2097152 | tf_op jit(solution)/shard_map/merge/pallas_call | solution.py:349
  57.7 0.0 copy-done.1
  57.8 0.0 copy-done.2
  57.8 1.3 %fusion.1 = bf16[256,2048]{1,0:T(8,128)(2,1)} fusion(f32[2,4,2,16,2048]{4,3,2,1,0:T(8,128)S(1)} %merge.1, bf16[256,2048]{1,0:T(8,128)(2,1)S(1)} %copy-done.1, f32[2048]{0:T(1024)S(1)} %copy-done.2), kind=kLoop, calls=%fused_computation.2 | loop fusion | flops 2097152 | bytes 4202496 | tf_op jit(solution)/shard_map/convert_element_type | solution.py:374
Async XLA Ops:
  0.6 25.2 %copy-start = (bf16[512,2048]{1,0:T(8,128)(2,1)S(1)}, bf16[512,2048]{1,0:T(8,128)(2,1)}, u32[]{:S(2)}) copy-start(bf16[512,2048]{1,0:T(8,128)(2,1)} %wo.1) | copy-start | bytes 6291460
  25.9 31.9 %copy-start.1 = (bf16[256,2048]{1,0:T(8,128)(2,1)S(1)}, bf16[256,2048]{1,0:T(8,128)(2,1)}, u32[]{:S(2)}) copy-start(bf16[256,2048]{1,0:T(8,128)(2,1)} %hid_h.1) | copy-start | bytes 3145732
  25.9 31.9 %copy-start.2 = (f32[2048]{0:T(1024)S(1)}, f32[2048]{0:T(1024)}, u32[]{:S(2)}) copy-start(f32[2048]{0:T(1024)} %param.23) | copy-start | bytes 24580

commit v6 on v4

--- a/solution.py
+++ b/solution.py
@@ -13,7 +13,7 @@
 DEPTH = 8
 EARLY = 3
 GROUPS = 2
-LOW = -1e30
+LOW = float(jnp.finfo(F32).min)
 
 
 def attend_kernel(n_sq, lens, hid_h, gain, bias, wq_h, bq, wkv_h, bkv, k_in, v_in,

time: 58.9 us -> 58.9 us (level)
  no operation moved by 1% of the time
where the time goes in v6:
time: 58.9 us
  Pallas kernels  56.9 us (97%)
  other arithmetic  1.29 us (2%)
  between operations  0.7 us (1%)
    pallas_call x1, Pallas kernels, merge(): pl.pallas_call(functools.partial(merge_kernel, n_tp, n_sq, heads), in_spe...  31.7 us
    pallas_call x1, Pallas kernels, attend(): pl.pallas_call(functools.partial(attend_kernel, n_sq), in_specs=[SM, ANYW...  25.2 us
    convert_element_type x1, other arithmetic, local_step(): (hidden.astype(F32) + y.reshape(hidden.shape) + b_out).astype(BF16)  1.29 us

profile of v6, /device:TPU:97, one launch (start us, length us, event | category | flops | bytes accessed | tf_op | source)
XLA Modules:
  0.0 58.9 jit_solution(8176002691162954065)
XLA Ops:
  0.6 0.0 copy-start
  0.6 25.2 %attend.1 = (bf16[256,256,128]{2,1,0:T(8,128)(2,1)}, bf16[256,256,128]{2,1,0:T(8,128)(2,1)}, f32[2,8,72,128]{3,2,1,0:T(8,128)S(1)}) custom-call(s32[256]{0:T(256)} %lens.1, bf16[256,2048]{1,0:T(8,128)(2,1)} %hid_h.1, f32[1,2048]{1,0:T(1,128)} %bitcast.12, f32[1,2048]{1,0:T(1,128)} %bitcast.13, bf16[2048,512]{1,0:T(8,128)(2,1)} %wq_h.1, f32[1,512]{1,0:T(1,128)} %bitcast.14, ...), custom_call_target="tpu_custom_call" | custom-call | flops 268435456 | bytes 33554432 | tf_op jit(solution)/shard_map/attend/pallas_call | solution.py:320
  25.9 0.0 copy-done
  25.9 0.0 copy-start.1
  25.9 0.0 copy-start.2
  25.9 31.7 %merge.1 = f32[2,4,2,16,2048]{4,3,2,1,0:T(8,128)S(1)} custom-call(f32[2,4,2,72,128]{4,3,2,1,0:T(8,128)S(1)} %bitcast.11, bf16[512,2048]{1,0:T(8,128)(2,1)S(1)} %copy-done), custom_call_target="tpu_custom_call" | custom-call | flops 1342177280 | bytes 2097152 | tf_op jit(solution)/shard_map/merge/pallas_call | solution.py:349
  57.6 0.0 copy-done.1
  57.6 0.0 copy-done.2
  57.6 1.3 %fusion.1 = bf16[256,2048]{1,0:T(8,128)(2,1)} fusion(f32[2,4,2,16,2048]{4,3,2,1,0:T(8,128)S(1)} %merge.1, bf16[256,2048]{1,0:T(8,128)(2,1)S(1)} %copy-done.1, f32[2048]{0:T(1024)S(1)} %copy-done.2), kind=kLoop, calls=%fused_computation.2 | loop fusion | flops 2097152 | bytes 4202496 | tf_op jit(solution)/shard_map/convert_element_type | solution.py:374
Async XLA Ops:
  0.6 25.2 %copy-start = (bf16[512,2048]{1,0:T(8,128)(2,1)S(1)}, bf16[512,2048]{1,0:T(8,128)(2,1)}, u32[]{:S(2)}) copy-start(bf16[512,2048]{1,0:T(8,128)(2,1)} %wo.1) | copy-start | bytes 6291460
  25.9 31.7 %copy-start.1 = (bf16[256,2048]{1,0:T(8,128)(2,1)S(1)}, bf16[256,2048]{1,0:T(8,128)(2,1)}, u32[]{:S(2)}) copy-start(bf16[256,2048]{1,0:T(8,128)(2,1)} %hid_h.1) | copy-start | bytes 3145732
  25.9 31.7 %copy-start.2 = (f32[2048]{0:T(1024)S(1)}, f32[2048]{0:T(1024)}, u32[]{:S(2)}) copy-start(f32[2048]{0:T(1024)} %param.23) | copy-start | bytes 24580
